TPU v7x, 32 devices: a whole 2x2x4 slice. The times are simulated.
32 devices in a mesh: grp: 4 (over z), sp: 8 (over y, x, core).
Axes of the slice: x: 2, y: 2, z: 4, core: 2. Of those that a mesh axis runs over, the one named last changes fastest.
Arguments:
- tokens: bfloat16 [2048, 2880], P(('grp', 'sp')), may hold values from -36 to 36
- query_weight: bfloat16 [2880, 2048], P(None, 'sp'), may hold values from -0.109375 to 0.109375
- key_value_weight: bfloat16 [2880, 1024], replicated, may hold values from -0.109375 to 0.109375
- block_places: int32 [16], replicated, may hold values from 0 to 15, each once
- sinks: float32 [32], replicated, may hold values from -1 to 5
Outputs:
- attended: bfloat16 [2048, 2048], P(('grp', 'sp'))
Inputs may be any that keep to these rules, and one draw needn't show every extreme that they name: `block_places`: every sequence block appears once.
All inputs are finite; a program needn't handle non-finite values.
Results may differ from a plain program's by a relative error of at most 0.008.
The roundings to bfloat16 on the way count: a program that leaves them out, or rounds other values in their place, can miss the bound.
Values may be sent and summed in bfloat16 or wider, within the bound.
A program may use at most 128 MiB of HBM per device.

v0:
```python
import jax
import jax.numpy as jnp
from jax import lax
from jax.sharding import PartitionSpec as P

QUERY_HEADS = 32
HEAD_SIZE = 64
BPG = 4
rope_base = 150000.0
neg_large = -1e30


def rotate(vectors, angles):
    middle = vectors.shape[-1] // 2
    first_half = vectors[..., :middle]
    second_half = vectors[..., middle:]
    cosine = jnp.cos(angles)
    sine_part = jnp.sin(angles)
    return jnp.concatenate(
        [
            first_half * cosine - second_half * sine_part,
            second_half * cosine + first_half * sine_part,
        ],
        axis=-1,
    )


def locate(stored, block_rows, block_places):
    blocks = stored // block_rows
    table = jnp.arange(block_places.shape[0], dtype=jnp.int32)
    onehot = (blocks[:, None] == table[None, :]).astype(jnp.int32)
    return jnp.sum(onehot * block_places[None, :], axis=1) * block_rows + stored % block_rows


def prepare(projected, own_places, query_cols, kv_cols, head_count):
    row_count = projected.shape[0]
    inverse = rope_base ** (-(jnp.arange(HEAD_SIZE // 2, dtype=jnp.float32) * 2.0) / HEAD_SIZE)
    angles = own_places.astype(jnp.float32)[:, None, None] * inverse[None, None, :]
    queries = rotate(
        projected[:, :query_cols].reshape(row_count, query_cols // HEAD_SIZE, HEAD_SIZE), angles
    ).astype(jnp.bfloat16)
    rotated_keys = rotate(
        projected[:, query_cols : query_cols + kv_cols].reshape(row_count, head_count, HEAD_SIZE),
        angles,
    )
    key_value_pair = jnp.concatenate(
        [rotated_keys.reshape(row_count, kv_cols), projected[:, query_cols + kv_cols :]], axis=1
    ).astype(jnp.bfloat16)
    return (queries, key_value_pair)


def attend(state, queries, query_places, key_value_pair, key_places, head_count):
    maxima, totals, mixture = state
    key_count = key_value_pair.shape[0]
    column_half = key_value_pair.shape[1] // 2
    key_part = key_value_pair[:, :column_half].reshape(key_count, head_count, HEAD_SIZE)
    value_part = key_value_pair[:, column_half:].reshape(key_count, head_count, HEAD_SIZE)
    scores = jnp.einsum(
        "qhgd,khd->hgqk", queries, key_part, preferred_element_type=jnp.float32
    ) * HEAD_SIZE ** (-0.5)
    allowed = key_places[None, :] <= query_places[:, None]
    scores = jnp.where(allowed, scores, neg_large)
    updated = jnp.maximum(maxima, jnp.max(scores, axis=-1))
    weights = jnp.where(allowed, jnp.exp(scores - updated[..., None]), 0.0)
    factor = jnp.exp(maxima - updated)
    totals = totals * factor + jnp.sum(weights, axis=-1)
    mixture = mixture * factor[..., None] + jnp.einsum(
        "hgqk,khd->hgqd",
        weights.astype(jnp.bfloat16),
        value_part,
        preferred_element_type=jnp.float32,
    )
    return (updated, totals, mixture)


def per_device(tokens, query_weight, key_value_weight, block_places, sinks):
    sp_count = lax.axis_size("sp")
    local_rows = tokens.shape[0]
    group_rows = local_rows * sp_count
    block_rows = group_rows // BPG
    kv_total = key_value_weight.shape[1] // (2 * HEAD_SIZE)
    sp_place = lax.axis_index("sp")
    grp_place = lax.axis_index("grp")
    query_cols = query_weight.shape[1]
    query_heads = query_cols // HEAD_SIZE
    head_count = max(kv_total // sp_count, 1)
    kv_cols = head_count * HEAD_SIZE
    first_head = sp_place * query_heads // (QUERY_HEADS // kv_total)
    key_weight = lax.dynamic_slice_in_dim(key_value_weight, first_head * HEAD_SIZE, kv_cols, 1)
    value_weight = lax.dynamic_slice_in_dim(
        key_value_weight, kv_total * HEAD_SIZE + first_head * HEAD_SIZE, kv_cols, 1
    )
    joined = jnp.concatenate([query_weight, key_weight, value_weight], axis=1)
    projected = jnp.dot(
        lax.all_gather(tokens, "sp", axis=0, tiled=True), joined, preferred_element_type=jnp.float32
    )
    query_local = jnp.arange(group_rows, dtype=jnp.int32)
    head_first = sp_place * query_heads
    own_places = locate(grp_place * group_rows + query_local, block_rows, block_places)
    queries, key_value_pair = prepare(projected, own_places, query_cols, kv_cols, head_count)
    query_sharing = query_heads // head_count
    head_sinks = lax.dynamic_slice_in_dim(sinks, head_first, query_heads, 0).reshape(
        head_count, query_sharing
    )
    sink_rows = jnp.broadcast_to(head_sinks[:, :, None], (head_count, query_sharing, group_rows))
    query_block4 = queries.reshape(group_rows, head_count, query_sharing, HEAD_SIZE)
    initial = (
        sink_rows,
        jnp.ones((head_count, query_sharing, group_rows), jnp.float32),
        jnp.zeros((head_count, query_sharing, group_rows, HEAD_SIZE), jnp.float32),
    )
    piece = lax.all_gather(key_value_pair, "grp", axis=0, tiled=True)
    step_rows = min(piece.shape[0], group_rows)
    turns = piece.shape[0] // step_rows

    def visit(turn, inner):
        offset = turn * step_rows
        piece_rows = lax.dynamic_slice_in_dim(piece, offset, step_rows, 0)
        position = offset + jnp.arange(step_rows, dtype=jnp.int32)
        stored = position // group_rows * group_rows + position % group_rows
        key_places = locate(stored, block_rows, block_places)
        return attend(inner, query_block4, own_places, piece_rows, key_places, head_count)

    maxima, totals, mixture = lax.fori_loop(0, turns, visit, initial)
    normed = jnp.transpose(mixture, (2, 0, 1, 3)) / jnp.transpose(totals, (2, 0, 1))[..., None]
    attended = normed.reshape(group_rows, query_cols).astype(jnp.bfloat16)
    return lax.all_to_all(attended, "sp", split_axis=0, concat_axis=1, tiled=True)


def solution(mesh):
    in_specs = (P(("grp", "sp"), None), P(None, "sp"), P(), P(), P())
    out_specs = P(("grp", "sp"), None)
    return jax.shard_map(
        per_device, mesh=mesh, in_specs=in_specs, out_specs=out_specs, check_vma=False
    )
```

profile of v0, /device:TPU:0, one launch (start us, length us, event | category | flops | bytes accessed | tf_op | source)
XLA Modules:
  0.0 114.0 jit_solution(16821734951300925589)
XLA Ops:
  6.5 0.0 all-gather.2.cloned.1.call-start
  6.5 0.7 all-gather.2.cloned.1.call-update
  7.3 0.7 dynamic_slice.20
  8.1 0.7 select_reduce_fusion.1
  8.8 0.3 multiply_cosine_fusion
  9.1 1.8 %constant_dynamic-slice_fusion.1 = (bf16[2880,64]{1,0:T(8,128)(2,1)S(1)}, bf16[2880,64]{1,0:T(8,128)(2,1)S(1)}) fusion(bf16[2880,1024]{1,0:T(8,128)(2,1)} %param.9, s32[]{:T(128)S(6)} %select_n.163, s32[]{:T(128)S(6)} %select_n.164), kind=kLoop, calls=%fused_computation.92 | loop fusion | bytes 1474568 | tf_op jit(solution)/shard_map/dynamic_slice | solution.py:89
  11.0 32.6 %all-gather.2.cloned.1.call-done = bf16[512,2880]{1,0:T(8,128)(2,1)} async-done(((bf16[64,2880]{1,0:T(8,128)(2,1)}), bf16[512,2880]{1,0:T(8,128)(2,1)}) %all-gather.2.cloned.1.call-update) | async-done | bytes 2949136 | tf_op jit(solution)/shard_map/all_gather | solution.py:95
  43.6 0.0 copy-start.1
  43.6 4.1 %fusion.32 = f32[512,384]{0,1:T(8,128)S(1)} fusion(bf16[512,2880]{1,0:T(8,128)(2,1)} %all-gather.2.cloned.1.call-done, bf16[2880,64]{1,0:T(8,128)(2,1)S(1)} %get-tuple-element.296, bf16[2880,64]{1,0:T(8,128)(2,1)S(1)} %get-tuple-element.295, bf16[2880,256]{1,0:T(8,128)(2,1)} %param.8), kind=kOutput, calls=%fused_computation.53 | convolution fusion | flops 1139097600 | bytes 5947392 | tf_op jit(solution)/shard_map/dot_general | solution.py:94
  47.8 0.3 fusion.43
  48.2 16.0 %all_gather.7 = bf16[2048,128]{0,1:T(8,128)(2,1)S(1)} all-gather(bf16[512,128]{0,1:T(8,128)(2,1)S(1)} %pad_maximum_fusion.1), channel_id=1, replica_groups=mesh['grp'=4,'sp'=8] {'grp'}, dimensions={0}, use_global_device_ids=true | all-gather | bytes 655360 | tf_op jit(solution)/shard_map/all_gather | solution.py:112
  64.2 0.1 fusion.36
  64.3 0.1 broadcast_in_dim.74
  64.4 0.0 copy-done.1
  64.4 31.9 %while.21 = (s32[]{:T(128)}, f32[1,4,512]{2,1,0:T(4,128)S(1)}, f32[1,4,512]{2,1,0:T(4,128)S(1)}, f32[1,4,512,64]{2,3,1,0:T(8,128)S(1)}, s32[16]{0:T(128)S(1)}, /...) while((s32[]{:T(128)}, f32[1,4,512]{2,1,0:T(4,128)S(1)}, ...), condition=%wide.region_5.6_spmd.clone, body=%wide.region_1.5_spmd.clone.sunk | while | flops 282791424 | bytes 31996208 | solution.py:124
  64.4 0.1 select_reduce_fusion.3
  64.5 0.2 broadcast_compare_fusion.3
  64.7 2.8 %fusion.62 = (f32[4,512]{1,0:T(4,128)S(1)}, f32[512,512,4]{1,0,2:T(8,128)}) fusion(pred[512,512]{0,1:T(8,128)(4,1)S(1)} %broadcast_compare_fusion.3, bf16[512,1,4,64]{0,3,2,1:T(8,128)(2,1)S(1)} %get-tuple-element.393, bf16[2048,128]{0,1:T(8,128)(2,1)S(1)} %get-tuple-element.392, s32[]{:T(128)S(6)} %select_n.256), kind=kOutput, calls=%fused_computation.2.clone.1 | convolution fusion | flops 137361408 | bytes 4792324 | tf_op jit(solution)/shard_map/while/body/eval_jaxpr/qhgd,khd->hgqk/dot_general | solution.py:58
  67.5 0.0 copy-start
  67.6 3.7 %fusion.65 = f32[1,4,512,64]{2,3,1,0:T(8,128)S(1)} fusion(f32[512,512,4]{1,0,2:T(8,128)} %get-tuple-element.358, f32[4,512]{1,0:T(4,128)S(1)} %bitcast.99, pred[512,512]{0,1:T(8,128)(4,1)S(1)} %broadcast_compare_fusion.3, f32[1,4,512,64]{2,3,1,0:T(8,128)S(1)} %get-tuple-element.376, f32[4,512]{1,0:T(4,128)S(1)} %get-tuple-element.359, ...), kind=kOutput, calls=%fused_computation.9.clone.1 | convolution fusion | flops 139853824 | bytes 5586953 | tf_op jit(solution)/shard_map/while/body/eval_jaxpr/hgqk,khd->hgqd/dot_general | solution.py:67
  71.3 0.0 copy-done
  71.3 1.0 fusion.64
  72.4 0.1 select_reduce_fusion.3
  72.5 0.2 broadcast_compare_fusion.3
  72.7 2.8 %fusion.62 = (f32[4,512]{1,0:T(4,128)S(1)}, f32[512,512,4]{1,0,2:T(8,128)}) fusion(pred[512,512]{0,1:T(8,128)(4,1)S(1)} %broadcast_compare_fusion.3, bf16[512,1,4,64]{0,3,2,1:T(8,128)(2,1)S(1)} %get-tuple-element.393, bf16[2048,128]{0,1:T(8,128)(2,1)S(1)} %get-tuple-element.392, s32[]{:T(128)S(6)} %select_n.256), kind=kOutput, calls=%fused_computation.2.clone.1 | convolution fusion | flops 137361408 | bytes 4792324 | tf_op jit(solution)/shard_map/while/body/eval_jaxpr/qhgd,khd->hgqk/dot_general | solution.py:58
  75.5 0.0 copy-start
  75.6 3.7 %fusion.65 = f32[1,4,512,64]{2,3,1,0:T(8,128)S(1)} fusion(f32[512,512,4]{1,0,2:T(8,128)} %get-tuple-element.358, f32[4,512]{1,0:T(4,128)S(1)} %bitcast.99, pred[512,512]{0,1:T(8,128)(4,1)S(1)} %broadcast_compare_fusion.3, f32[1,4,512,64]{2,3,1,0:T(8,128)S(1)} %get-tuple-element.376, f32[4,512]{1,0:T(4,128)S(1)} %get-tuple-element.359, ...), kind=kOutput, calls=%fused_computation.9.clone.1 | convolution fusion | flops 139853824 | bytes 5586953 | tf_op jit(solution)/shard_map/while/body/eval_jaxpr/hgqk,khd->hgqd/dot_general | solution.py:67
  79.3 0.0 copy-done
  79.3 1.0 fusion.64
  80.4 0.1 select_reduce_fusion.3
  80.5 0.2 broadcast_compare_fusion.3
  80.7 2.8 %fusion.62 = (f32[4,512]{1,0:T(4,128)S(1)}, f32[512,512,4]{1,0,2:T(8,128)}) fusion(pred[512,512]{0,1:T(8,128)(4,1)S(1)} %broadcast_compare_fusion.3, bf16[512,1,4,64]{0,3,2,1:T(8,128)(2,1)S(1)} %get-tuple-element.393, bf16[2048,128]{0,1:T(8,128)(2,1)S(1)} %get-tuple-element.392, s32[]{:T(128)S(6)} %select_n.256), kind=kOutput, calls=%fused_computation.2.clone.1 | convolution fusion | flops 137361408 | bytes 4792324 | tf_op jit(solution)/shard_map/while/body/eval_jaxpr/qhgd,khd->hgqk/dot_general | solution.py:58
  83.5 0.0 copy-start
  83.5 3.7 %fusion.65 = f32[1,4,512,64]{2,3,1,0:T(8,128)S(1)} fusion(f32[512,512,4]{1,0,2:T(8,128)} %get-tuple-element.358, f32[4,512]{1,0:T(4,128)S(1)} %bitcast.99, pred[512,512]{0,1:T(8,128)(4,1)S(1)} %broadcast_compare_fusion.3, f32[1,4,512,64]{2,3,1,0:T(8,128)S(1)} %get-tuple-element.376, f32[4,512]{1,0:T(4,128)S(1)} %get-tuple-element.359, ...), kind=kOutput, calls=%fused_computation.9.clone.1 | convolution fusion | flops 139853824 | bytes 5586953 | tf_op jit(solution)/shard_map/while/body/eval_jaxpr/hgqk,khd->hgqd/dot_general | solution.py:67
  87.2 0.0 copy-done
  87.3 1.0 fusion.64
  88.4 0.1 select_reduce_fusion.3
  88.5 0.2 broadcast_compare_fusion.3
  88.7 2.8 %fusion.62 = (f32[4,512]{1,0:T(4,128)S(1)}, f32[512,512,4]{1,0,2:T(8,128)}) fusion(pred[512,512]{0,1:T(8,128)(4,1)S(1)} %broadcast_compare_fusion.3, bf16[512,1,4,64]{0,3,2,1:T(8,128)(2,1)S(1)} %get-tuple-element.393, bf16[2048,128]{0,1:T(8,128)(2,1)S(1)} %get-tuple-element.392, s32[]{:T(128)S(6)} %select_n.256), kind=kOutput, calls=%fused_computation.2.clone.1 | convolution fusion | flops 137361408 | bytes 4792324 | tf_op jit(solution)/shard_map/while/body/eval_jaxpr/qhgd,khd->hgqk/dot_general | solution.py:58
  91.5 0.0 copy-start
  91.5 3.7 %fusion.65 = f32[1,4,512,64]{2,3,1,0:T(8,128)S(1)} fusion(f32[512,512,4]{1,0,2:T(8,128)} %get-tuple-element.358, f32[4,512]{1,0:T(4,128)S(1)} %bitcast.99, pred[512,512]{0,1:T(8,128)(4,1)S(1)} %broadcast_compare_fusion.3, f32[1,4,512,64]{2,3,1,0:T(8,128)S(1)} %get-tuple-element.376, f32[4,512]{1,0:T(4,128)S(1)} %get-tuple-element.359, ...), kind=kOutput, calls=%fused_computation.9.clone.1 | convolution fusion | flops 139853824 | bytes 5586953 | tf_op jit(solution)/shard_map/while/body/eval_jaxpr/hgqk,khd->hgqd/dot_general | solution.py:67
  95.2 0.0 copy-done
  95.3 1.0 fusion.64
  96.3 0.1 fusion.35
  96.4 0.3 convert_element_type.40
  96.7 0.3 copy.15
  97.0 9.4 %all_to_all.16 = bf16[8,64,256]{2,1,0:T(8,128)(2,1)S(1)} all-to-all(bf16[8,64,256]{2,1,0:T(8,128)(2,1)S(1)} %copy.15), channel_id=1, replica_groups=mesh['grp'=4,'sp'=8] {'sp'}, dimensions={0} | all-to-all | bytes 524288 | tf_op jit(solution)/shard_map/all_to_all | solution.py:127
  106.5 0.7 copy.18
  (31 shorter events, 0.4 us)
Async XLA Ops:
  6.5 37.1 %all-gather.2.cloned.1.call-start = ((), (), s32[]{:S(2)}) async-start(), calls=%async_computation.1 | async-start | bytes 3391488 | tf_op jit(solution)/shard_map/all_gather | solution.py:95
  43.6 20.8 %copy-start.1 = (s32[16]{0:T(128)S(1)}, s32[16]{0:T(128)}, u32[]{:S(2)}) copy-start(s32[16]{0:T(128)} %param.10) | copy-start | bytes 196
  67.5 3.7 %copy-start = (f32[512,512,4]{1,0,2:T(8,128)S(1)}, f32[512,512,4]{1,0,2:T(8,128)}, u32[]{:S(2)}) copy-start(f32[512,512,4]{1,0,2:T(8,128)} %get-tuple-element.358) | copy-start | bytes 12582916 | tf_op jit(solution)/shard_map/while
  75.5 3.7 %copy-start = (f32[512,512,4]{1,0,2:T(8,128)S(1)}, f32[512,512,4]{1,0,2:T(8,128)}, u32[]{:S(2)}) copy-start(f32[512,512,4]{1,0,2:T(8,128)} %get-tuple-element.358) | copy-start | bytes 12582916 | tf_op jit(solution)/shard_map/while
  83.5 3.7 %copy-start = (f32[512,512,4]{1,0,2:T(8,128)S(1)}, f32[512,512,4]{1,0,2:T(8,128)}, u32[]{:S(2)}) copy-start(f32[512,512,4]{1,0,2:T(8,128)} %get-tuple-element.358) | copy-start | bytes 12582916 | tf_op jit(solution)/shard_map/while
  91.5 3.7 %copy-start = (f32[512,512,4]{1,0,2:T(8,128)S(1)}, f32[512,512,4]{1,0,2:T(8,128)}, u32[]{:S(2)}) copy-start(f32[512,512,4]{1,0,2:T(8,128)} %get-tuple-element.358) | copy-start | bytes 12582916 | tf_op jit(solution)/shard_map/while
Sparse Core Ops, SparseCore 0:
  9.2 34.3 all-gather.1
where the time goes:
time: 114 us
  waiting for transfers between devices  33.3 us (29%)
  matrix products  30.1 us (26%)
  blocking collectives  25.5 us (22%)
  between operations  13.6 us (12%)
  other arithmetic  7.27 us (6%)
  local copies, waits for them, and re-layouts  4.05 us (4%)
    all_gather x1, waiting for transfers between devices, per_device(): lax.all_gather(tokens, 'sp', axis=0, tiled=True)  32.6 us
    all_gather x1, blocking collectives, per_device(): piece = lax.all_gather(key_value_pair, 'grp', axis=0, tiled=True)  16 us
    dot_general x4, matrix products, attend(): jnp.einsum('hgqk,khd->hgqd', weights.astype(jnp.bfloat16), value_part, pr...  14.8 us
    dot_general x4, matrix products, attend(): jnp.einsum('qhgd,khd->hgqk', queries, key_part, preferred_element_type=jn...  11.2 us
    all_to_all x1, blocking collectives, per_device(): lax.all_to_all(attended, 'sp', split_axis=0, concat_axis=1, tiled=True)  9.44 us
    reduce_sum x4, other arithmetic, attend(): totals = totals * factor + jnp.sum(weights, axis=-1)  4.17 us
    dot_general x1, matrix products, per_device(): jnp.dot(lax.all_gather(tokens, 'sp', axis=0, tiled=True), joined, preferr...  4.11 us
  transfers between devices with their start and end apart: 1, of which 1 were waited for; matrix products, arithmetic and copies ran while one was open for 3% of the time, Pallas kernels for 0%

commit v1 on v0

--- a/solution.py
+++ b/solution.py
@@ -109,7 +109,12 @@
         jnp.ones((head_count, query_sharing, group_rows), jnp.float32),
         jnp.zeros((head_count, query_sharing, group_rows, HEAD_SIZE), jnp.float32),
     )
-    piece = lax.all_gather(key_value_pair, "grp", axis=0, tiled=True)
+    ring = [key_value_pair]
+    for hop in range(3):
+        ring.append(lax.ppermute(ring[-1], "grp", [(dev, (dev + 1) % 4) for dev in range(4)]))
+    piece = jnp.roll(
+        jnp.concatenate(ring[::-1], axis=0), (lax.axis_index("grp") + 1) * ring[0].shape[0], axis=0
+    )
     step_rows = min(piece.shape[0], group_rows)
     turns = piece.shape[0] // step_rows
 

time: 114 us -> 119 us (1.044)
  waiting for transfers between devices: 33.3 us -> 53.4 us
  blocking collectives: 25.5 us -> 9.44 us
  starting transfers between devices: 0.01 us -> 1.54 us
    ppermute x0 -> x3, waiting for transfers between devices: none -> 18.9 us  [per_device(): lax.ppermute(ring[-1], 'grp', [(dev, (dev + 1) % 4) for dev in range(4)])]
    all_gather x1 -> x0, blocking collectives: 16 us -> none  [per_device(): piece = lax.all_gather(key_value_pair, 'grp', axis=0, tiled=True)]
    ppermute x0 -> x3, starting transfers between devices: none -> 1.54 us  [per_device(): lax.ppermute(ring[-1], 'grp', [(dev, (dev + 1) % 4) for dev in range(4)])]
  transfers between devices with their start and end apart: 1 -> 4, of which waited for: 1 -> 4; matrix products, arithmetic and copies ran while one was open for 3% -> 3% of each run, Pallas kernels for 0% -> 0%
where the time goes in v1:
time: 119 us
  waiting for transfers between devices  53.4 us (45%)
  matrix products  30.1 us (25%)
  between operations  13.6 us (11%)
  blocking collectives  9.44 us (8%)
  other arithmetic  7.29 us (6%)
  local copies, waits for them, and re-layouts  3.49 us (3%)
  starting transfers between devices  1.54 us (1%)
    all_gather x1, waiting for transfers between devices, per_device(): lax.all_gather(tokens, 'sp', axis=0, tiled=True)  33.7 us
    ppermute x3, waiting for transfers between devices, per_device(): lax.ppermute(ring[-1], 'grp', [(dev, (dev + 1) % 4) for dev in range(4)])  18.9 us
    dot_general x4, matrix products, attend(): jnp.einsum('hgqk,khd->hgqd', weights.astype(jnp.bfloat16), value_part, pr...  14.8 us
    dot_general x4, matrix products, attend(): jnp.einsum('qhgd,khd->hgqk', queries, key_part, preferred_element_type=jn...  11.1 us
    all_to_all x1, blocking collectives, per_device(): lax.all_to_all(attended, 'sp', split_axis=0, concat_axis=1, tiled=True)  9.44 us
    reduce_sum x4, other arithmetic, attend(): totals = totals * factor + jnp.sum(weights, axis=-1)  4.17 us
    dot_general x1, matrix products, per_device(): jnp.dot(lax.all_gather(tokens, 'sp', axis=0, tiled=True), joined, preferr...  4.1 us
  transfers between devices with their start and end apart: 4, of which 4 were waited for; matrix products, arithmetic and copies ran while one was open for 3% of the time, Pallas kernels for 0%

profile of v1, /device:TPU:0, one launch (start us, length us, event | category | flops | bytes accessed | tf_op | source)
XLA Modules:
  0.0 119.1 jit_solution(15063231160592752952)
XLA Ops:
  6.5 0.7 all-gather.2.cloned.1.call-update
  7.3 0.7 select_reduce_fusion.1
  8.1 1.8 %constant_dynamic-slice_fusion.2 = (bf16[2880,64]{1,0:T(8,128)(2,1)S(1)}, bf16[2880,64]{1,0:T(8,128)(2,1)S(1)}) fusion(bf16[2880,1024]{1,0:T(8,128)(2,1)} %param.9, s32[]{:T(128)S(6)} %select_n.175, s32[]{:T(128)S(6)} %select_n.176), kind=kLoop, calls=%fused_computation.100 | loop fusion | bytes 1474568 | tf_op jit(solution)/shard_map/dynamic_slice | solution.py:89
  9.9 33.7 %all-gather.2.cloned.1.call-done = bf16[512,2880]{1,0:T(8,128)(2,1)} async-done(((bf16[64,2880]{1,0:T(8,128)(2,1)}), bf16[512,2880]{1,0:T(8,128)(2,1)}) %all-gather.2.cloned.1.call-update) | async-done | bytes 2949136 | tf_op jit(solution)/shard_map/all_gather | solution.py:95
  43.6 4.1 %fusion.32 = f32[512,384]{0,1:T(8,128)S(1)} fusion(bf16[512,2880]{1,0:T(8,128)(2,1)} %all-gather.2.cloned.1.call-done, bf16[2880,64]{1,0:T(8,128)(2,1)S(1)} %get-tuple-element.296, bf16[2880,64]{1,0:T(8,128)(2,1)S(1)} %get-tuple-element.295, bf16[2880,256]{1,0:T(8,128)(2,1)} %param.8), kind=kOutput, calls=%fused_computation.53 | convolution fusion | flops 1139097600 | bytes 5947392 | tf_op jit(solution)/shard_map/dot_general | solution.py:94
  47.7 0.0 copy-start.1
  47.8 0.3 fusion.43
  48.1 1.5 %collective-permute-start = (bf16[512,128]{0,1:T(8,128)(2,1)S(1)}, bf16[512,128]{0,1:T(8,128)(2,1)S(1)}, u32[]{:S(2)}, u32[]{:S(2)}) collective-permute-start(bf16[512,128]{0,1:T(8,128)(2,1)S(1)} %pad_maximum_fusion.1), channel_id=1, source_target_pairs={{0,8},{8,16},{16,24},{24,0},{1,9},{9,17},{17,25},{25,1},{2,10},{10... | collective-permute-start | bytes 393224 | tf_op jit(solution)/shard_map/ppermute | solution.py:114
  49.7 0.1 dynamic_slice.24
  49.7 5.9 %collective-permute-done = bf16[512,128]{0,1:T(8,128)(2,1)S(1)} collective-permute-done((bf16[512,128]{0,1:T(8,128)(2,1)S(1)}, bf16[512,128]{0,1:T(8,128)(2,1)S(1)}, u32[]{:S(2)}, u32[]{:S(2)}) %collective-permute-start) | collective-permute-done | bytes 131104 | tf_op jit(solution)/shard_map/ppermute | solution.py:114
  55.6 0.0 collective-permute-start.1
  55.6 0.3 multiply_cosine_fusion
  56.0 6.4 %collective-permute-done.1 = bf16[512,128]{0,1:T(8,128)(2,1)S(1)} collective-permute-done((bf16[512,128]{0,1:T(8,128)(2,1)S(1)}, bf16[512,128]{0,1:T(8,128)(2,1)S(1)}, u32[]{:S(2)}, u32[]{:S(2)}) %collective-permute-start.1) | collective-permute-done | bytes 131104 | tf_op jit(solution)/shard_map/ppermute | solution.py:114
  62.4 0.0 collective-permute-start.2
  62.4 0.1 fusion.36
  62.5 6.7 %collective-permute-done.2 = bf16[512,128]{0,1:T(8,128)(2,1)S(1)} collective-permute-done((bf16[512,128]{0,1:T(8,128)(2,1)S(1)}, bf16[512,128]{0,1:T(8,128)(2,1)S(1)}, u32[]{:S(2)}, u32[]{:S(2)}) %collective-permute-start.2) | collective-permute-done | bytes 131104 | tf_op jit(solution)/shard_map/ppermute | solution.py:114
  69.3 0.1 broadcast_in_dim.74
  69.4 0.0 copy-done.1
  69.4 32.0 %while.21 = (s32[]{:T(128)}, f32[1,4,512]{2,1,0:T(4,128)S(1)}, f32[1,4,512]{2,1,0:T(4,128)S(1)}, f32[1,4,512,64]{2,3,1,0:T(8,128)S(1)}, s32[16]{0:T(128)S(1)}, /...) while((s32[]{:T(128)}, f32[1,4,512]{2,1,0:T(4,128)S(1)}, ...), condition=%wide.region_5.6_spmd.clone, body=%wide.region_1.5_spmd.clone.sunk | while | flops 282791424 | bytes 31996208 | solution.py:129
  69.4 0.1 select_reduce_fusion.3
  69.6 0.2 broadcast_compare_fusion.3
  69.8 2.8 %fusion.62 = (f32[4,512]{1,0:T(4,128)S(1)}, f32[512,512,4]{1,0,2:T(8,128)}) fusion(pred[512,512]{0,1:T(8,128)(4,1)S(1)} %broadcast_compare_fusion.3, bf16[512,1,4,64]{0,3,2,1:T(8,128)(2,1)S(1)} %get-tuple-element.393, bf16[2048,128]{0,1:T(8,128)(2,1)S(1)} %get-tuple-element.392, s32[]{:T(128)S(6)} %select_n.270), kind=kOutput, calls=%fused_computation.2.clone.1 | convolution fusion | flops 137361408 | bytes 4792324 | tf_op jit(solution)/shard_map/while/body/eval_jaxpr/qhgd,khd->hgqk/dot_general | solution.py:58
  72.6 0.0 copy-start
  72.6 3.7 %fusion.65 = f32[1,4,512,64]{2,3,1,0:T(8,128)S(1)} fusion(f32[512,512,4]{1,0,2:T(8,128)} %get-tuple-element.358, f32[4,512]{1,0:T(4,128)S(1)} %bitcast.99, pred[512,512]{0,1:T(8,128)(4,1)S(1)} %broadcast_compare_fusion.3, f32[1,4,512,64]{2,3,1,0:T(8,128)S(1)} %get-tuple-element.376, f32[4,512]{1,0:T(4,128)S(1)} %get-tuple-element.359, ...), kind=kOutput, calls=%fused_computation.9.clone.1 | convolution fusion | flops 139853824 | bytes 5586953 | tf_op jit(solution)/shard_map/while/body/eval_jaxpr/hgqk,khd->hgqd/dot_general | solution.py:67
  76.3 0.0 copy-done
  76.3 1.0 fusion.64
  77.4 0.1 select_reduce_fusion.3
  77.5 0.2 broadcast_compare_fusion.3
  77.8 2.8 %fusion.62 = (f32[4,512]{1,0:T(4,128)S(1)}, f32[512,512,4]{1,0,2:T(8,128)}) fusion(pred[512,512]{0,1:T(8,128)(4,1)S(1)} %broadcast_compare_fusion.3, bf16[512,1,4,64]{0,3,2,1:T(8,128)(2,1)S(1)} %get-tuple-element.393, bf16[2048,128]{0,1:T(8,128)(2,1)S(1)} %get-tuple-element.392, s32[]{:T(128)S(6)} %select_n.270), kind=kOutput, calls=%fused_computation.2.clone.1 | convolution fusion | flops 137361408 | bytes 4792324 | tf_op jit(solution)/shard_map/while/body/eval_jaxpr/qhgd,khd->hgqk/dot_general | solution.py:58
  80.6 0.0 copy-start
  80.6 3.7 %fusion.65 = f32[1,4,512,64]{2,3,1,0:T(8,128)S(1)} fusion(f32[512,512,4]{1,0,2:T(8,128)} %get-tuple-element.358, f32[4,512]{1,0:T(4,128)S(1)} %bitcast.99, pred[512,512]{0,1:T(8,128)(4,1)S(1)} %broadcast_compare_fusion.3, f32[1,4,512,64]{2,3,1,0:T(8,128)S(1)} %get-tuple-element.376, f32[4,512]{1,0:T(4,128)S(1)} %get-tuple-element.359, ...), kind=kOutput, calls=%fused_computation.9.clone.1 | convolution fusion | flops 139853824 | bytes 5586953 | tf_op jit(solution)/shard_map/while/body/eval_jaxpr/hgqk,khd->hgqd/dot_general | solution.py:67
  84.3 1.0 fusion.64
  85.4 0.1 select_reduce_fusion.3
  85.5 0.2 broadcast_compare_fusion.3
  85.8 2.8 %fusion.62 = (f32[4,512]{1,0:T(4,128)S(1)}, f32[512,512,4]{1,0,2:T(8,128)}) fusion(pred[512,512]{0,1:T(8,128)(4,1)S(1)} %broadcast_compare_fusion.3, bf16[512,1,4,64]{0,3,2,1:T(8,128)(2,1)S(1)} %get-tuple-element.393, bf16[2048,128]{0,1:T(8,128)(2,1)S(1)} %get-tuple-element.392, s32[]{:T(128)S(6)} %select_n.270), kind=kOutput, calls=%fused_computation.2.clone.1 | convolution fusion | flops 137361408 | bytes 4792324 | tf_op jit(solution)/shard_map/while/body/eval_jaxpr/qhgd,khd->hgqk/dot_general | solution.py:58
  88.6 0.0 copy-start
  88.6 3.7 %fusion.65 = f32[1,4,512,64]{2,3,1,0:T(8,128)S(1)} fusion(f32[512,512,4]{1,0,2:T(8,128)} %get-tuple-element.358, f32[4,512]{1,0:T(4,128)S(1)} %bitcast.99, pred[512,512]{0,1:T(8,128)(4,1)S(1)} %broadcast_compare_fusion.3, f32[1,4,512,64]{2,3,1,0:T(8,128)S(1)} %get-tuple-element.376, f32[4,512]{1,0:T(4,128)S(1)} %get-tuple-element.359, ...), kind=kOutput, calls=%fused_computation.9.clone.1 | convolution fusion | flops 139853824 | bytes 5586953 | tf_op jit(solution)/shard_map/while/body/eval_jaxpr/hgqk,khd->hgqd/dot_general | solution.py:67
  92.3 1.0 fusion.64
  93.4 0.1 select_reduce_fusion.3
  93.5 0.2 broadcast_compare_fusion.3
  93.8 2.8 %fusion.62 = (f32[4,512]{1,0:T(4,128)S(1)}, f32[512,512,4]{1,0,2:T(8,128)}) fusion(pred[512,512]{0,1:T(8,128)(4,1)S(1)} %broadcast_compare_fusion.3, bf16[512,1,4,64]{0,3,2,1:T(8,128)(2,1)S(1)} %get-tuple-element.393, bf16[2048,128]{0,1:T(8,128)(2,1)S(1)} %get-tuple-element.392, s32[]{:T(128)S(6)} %select_n.270), kind=kOutput, calls=%fused_computation.2.clone.1 | convolution fusion | flops 137361408 | bytes 4792324 | tf_op jit(solution)/shard_map/while/body/eval_jaxpr/qhgd,khd->hgqk/dot_general | solution.py:58
  96.6 3.7 %fusion.65 = f32[1,4,512,64]{2,3,1,0:T(8,128)S(1)} fusion(f32[512,512,4]{1,0,2:T(8,128)} %get-tuple-element.358, f32[4,512]{1,0:T(4,128)S(1)} %bitcast.99, pred[512,512]{0,1:T(8,128)(4,1)S(1)} %broadcast_compare_fusion.3, f32[1,4,512,64]{2,3,1,0:T(8,128)S(1)} %get-tuple-element.376, f32[4,512]{1,0:T(4,128)S(1)} %get-tuple-element.359, ...), kind=kOutput, calls=%fused_computation.9.clone.1 | convolution fusion | flops 139853824 | bytes 5586953 | tf_op jit(solution)/shard_map/while/body/eval_jaxpr/hgqk,khd->hgqd/dot_general | solution.py:67
  100.3 1.0 fusion.64
  101.4 0.1 fusion.35
  101.4 0.3 convert_element_type.40
  101.7 0.3 copy.15
  102.1 9.4 %all_to_all.16 = bf16[8,64,256]{2,1,0:T(8,128)(2,1)S(1)} all-to-all(bf16[8,64,256]{2,1,0:T(8,128)(2,1)S(1)} %copy.15), channel_id=1, replica_groups=mesh['grp'=4,'sp'=8] {'sp'}, dimensions={0} | all-to-all | bytes 524288 | tf_op jit(solution)/shard_map/all_to_all | solution.py:132
  111.5 0.7 copy.18
  (47 shorter events, 0.6 us)
Async XLA Ops:
  6.5 37.1 %all-gather.2.cloned.1.call-start = ((), (), s32[]{:S(2)}) async-start(), calls=%async_computation.1 | async-start | bytes 3391488 | tf_op jit(solution)/shard_map/all_gather | solution.py:95
  43.6 6.1 %copy-start.2 = (f32[32]{0:T(128)S(1)}, f32[32]{0:T(128)}, u32[]{:S(2)}) copy-start(f32[32]{0:T(128)} %param.11) | copy-start | bytes 388
  47.7 21.7 %copy-start.1 = (s32[16]{0:T(128)S(1)}, s32[16]{0:T(128)}, u32[]{:S(2)}) copy-start(s32[16]{0:T(128)} %param.10) | copy-start | bytes 196
  48.1 7.5 %collective-permute-start = (bf16[512,128]{0,1:T(8,128)(2,1)S(1)}, bf16[512,128]{0,1:T(8,128)(2,1)S(1)}, u32[]{:S(2)}, u32[]{:S(2)}) collective-permute-start(bf16[512,128]{0,1:T(8,128)(2,1)S(1)} %pad_maximum_fusion.1), channel_id=1, source_target_pairs={{0,8},{8,16},{16,24},{24,0},{1,9},{9,17},{17,25},{25,1},{2,10},{10... | collective-permute-start | bytes 393224 | tf_op jit(solution)/shard_map/ppermute | solution.py:114
  55.6 6.8 %collective-permute-start.1 = (bf16[512,128]{0,1:T(8,128)(2,1)S(1)}, bf16[512,128]{0,1:T(8,128)(2,1)S(1)}, u32[]{:S(2)}, u32[]{:S(2)}) collective-permute-start(bf16[512,128]{0,1:T(8,128)(2,1)S(1)} %collective-permute-done), channel_id=1, source_target_pairs={{0,8},{8,16},{16,24},{24,0},{1,9},{9,17},{17,25},{25,1},{2,10},{10... | collective-permute-start | bytes 393224 | tf_op jit(solution)/shard_map/ppermute | solution.py:114
  62.4 6.8 %collective-permute-start.2 = (bf16[512,128]{0,1:T(8,128)(2,1)S(1)}, bf16[512,128]{0,1:T(8,128)(2,1)S(1)}, u32[]{:S(2)}, u32[]{:S(2)}) collective-permute-start(bf16[512,128]{0,1:T(8,128)(2,1)S(1)} %collective-permute-done.1), channel_id=1, source_target_pairs={{0,8},{8,16},{16,24},{24,0},{1,9},{9,17},{17,25},{25,1},{2,10},{10... | collective-permute-start | bytes 393224 | tf_op jit(solution)/shard_map/ppermute | solution.py:114
  72.6 3.7 %copy-start = (f32[512,512,4]{1,0,2:T(8,128)S(1)}, f32[512,512,4]{1,0,2:T(8,128)}, u32[]{:S(2)}) copy-start(f32[512,512,4]{1,0,2:T(8,128)} %get-tuple-element.358) | copy-start | bytes 12582916 | tf_op jit(solution)/shard_map/while
  80.6 3.7 %copy-start = (f32[512,512,4]{1,0,2:T(8,128)S(1)}, f32[512,512,4]{1,0,2:T(8,128)}, u32[]{:S(2)}) copy-start(f32[512,512,4]{1,0,2:T(8,128)} %get-tuple-element.358) | copy-start | bytes 12582916 | tf_op jit(solution)/shard_map/while
  88.6 3.7 %copy-start = (f32[512,512,4]{1,0,2:T(8,128)S(1)}, f32[512,512,4]{1,0,2:T(8,128)}, u32[]{:S(2)}) copy-start(f32[512,512,4]{1,0,2:T(8,128)} %get-tuple-element.358) | copy-start | bytes 12582916 | tf_op jit(solution)/shard_map/while
  96.6 3.7 %copy-start = (f32[512,512,4]{1,0,2:T(8,128)S(1)}, f32[512,512,4]{1,0,2:T(8,128)}, u32[]{:S(2)}) copy-start(f32[512,512,4]{1,0,2:T(8,128)} %get-tuple-element.358) | copy-start | bytes 12582916 | tf_op jit(solution)/shard_map/while
Sparse Core Ops, SparseCore 0:
  9.2 34.3 all-gather.1
